TPU v7x, 256 devices: a whole 4x4x8 slice. The times are simulated.
256 devices in a mesh: dp: 32 (over z, x_lo, core), tp: 8 (over y, x_hi).
Axes of the slice: x: 4 (x_hi: 2, x_lo: 2; x = x_hi * 2 + x_lo), y: 4, z: 8, core: 2. Of those that a mesh axis runs over, the one named last changes fastest.
Arguments:
- gate_pre: bfloat16 [24576, 7168], P('dp', 'tp'), may hold values from -6 to 6
- up_pre: bfloat16 [24576, 7168], P('dp', 'tp'), may hold values from -6 to 6
- target: bfloat16 [24576, 2048], P('dp', 'tp'), may hold values from -6 to 6
- norm_gain: float32 [2048], P('tp'), may hold values from 0.5 to 1.5
- weight: bfloat16 [32, 7168, 2048], P('dp', 'tp'), may hold values from -6 to 6
- round_index: int32 [1], replicated, may hold values from 0 to 9999
Outputs:
- normed: bfloat16 [24576, 2048], P('dp', 'tp')
- mixed: bfloat16 [32, 7168, 2048], P('dp', 'tp')
All inputs are finite; a program needn't handle non-finite values.
Results may differ from a plain program's by a relative error of at most 0.001.
The roundings to bfloat16 on the way count: a program that leaves them out, or rounds other values in their place, can miss the bound.
Values may be sent and summed in bfloat16 or wider, within the bound.
No kernel may reach another device: no remote copies, remote signals or barrier semaphores. Data moves between devices by JAX's collectives and lax.ppermute only.
A program may use at most 64 MiB of HBM per device.

v0:
```python
import functools
import math

import jax
import jax.numpy as jnp
from jax import lax
from jax.experimental import pallas as pl
from jax.experimental.pallas import tpu as pltpu
from jax.sharding import Mesh
from jax.sharding import PartitionSpec as P


FF = 7168
EPSILON = 1e-06
TP = ("tp_0", "tp_1")
BLOCK = 128
CODES = 16
F32, BF16 = jnp.float32, jnp.bfloat16

PLANS = (
    (0, 0, 224, True, True, False),
    (0, 0, 224, True, True, False),
    (0, 672, 224, False, False, True),
    (224, 336, 112, False, False, False),
    (0, 448, 224, True, False, False),
)


def step_rate(round_index):
    phase = (round_index[0] % 1000).astype(F32) * jnp.float32(2.0 * math.pi / 1000.0)
    return jnp.float32(0.25) * (jnp.float32(0.55) + jnp.float32(0.45) * jnp.cos(phase))


def columns_of(rows):
    filled = jnp.concatenate([rows, jnp.zeros((BLOCK - rows.shape[0], BLOCK), F32)], axis=0)
    return filled.T


def columns_at(number, width):
    return pl.ds(pl.multiple_of(number * width, width), width)


def forward_kernel(gate_ref, up_ref, weight_ref, hidden_t_ref, coded_ref, scale_scr, partial_scr):
    step = pl.program_id(0)
    hidden = jax.nn.silu(gate_ref[...].astype(F32)) * up_ref[...].astype(F32)
    hidden_t_ref[...] = hidden.T.astype(BF16)
    hidden = hidden.astype(BF16)
    parts, _, width = coded_ref.shape

    def products(number, top):
        weight = weight_ref[:, columns_at(number, 4 * width)]
        partial = jnp.dot(hidden, weight, preferred_element_type=F32) * FF ** (-0.5)
        for part in range(4):
            values = partial[:, part * width : (part + 1) * width]
            partial_scr[4 * number + part] = values
            for lanes in range(0, width, BLOCK):
                top = jnp.maximum(top, jnp.abs(values[:, lanes : lanes + BLOCK]))
        return top

    top = lax.fori_loop(0, parts // 4, products, jnp.zeros((BLOCK, BLOCK), F32))
    top = jnp.max(top, axis=1, keepdims=True)
    level = jnp.ceil(8.0 * jnp.log2(jnp.maximum(top, 1e-30))) + 1.0
    factor = jnp.exp2(15.0 - 0.125 * level)
    rows = pl.ds(pl.multiple_of(step * BLOCK, BLOCK), BLOCK)

    def coding(part, _):
        coded_ref[part, rows, :] = jnp.round(partial_scr[part] * factor).astype(jnp.int32).astype(jnp.int16)
        return 0

    lax.fori_loop(0, parts, coding, 0)
    scale_scr[pl.ds(step, 1), :] = jnp.broadcast_to(level, (BLOCK, BLOCK)).T[:1, :]

    @pl.when(step == pl.num_programs(0) - 1)
    def _():
        codes = scale_scr[...].astype(jnp.int32).astype(jnp.int16)
        tokens = coded_ref.shape[1] - CODES
        for part in range(parts):
            coded_ref[part, tokens:, :BLOCK] = codes
            coded_ref[part, tokens:, BLOCK:] = codes


def forward(gate, up, weight, parts):
    tokens, units = gate.shape
    width = weight.shape[1] // parts
    return pl.pallas_call(
        forward_kernel,
        grid=(tokens // BLOCK,),
        in_specs=[
            pl.BlockSpec((BLOCK, units), lambda i: (i, 0)),
            pl.BlockSpec((BLOCK, units), lambda i: (i, 0)),
            pl.BlockSpec(weight.shape, lambda i: (0, 0)),
        ],
        out_specs=[
            pl.BlockSpec((units, BLOCK), lambda i: (0, i)),
            pl.BlockSpec((parts, tokens + CODES, width), lambda i: (0, 0, 0)),
        ],
        out_shape=[
            jax.ShapeDtypeStruct((units, tokens), BF16),
            jax.ShapeDtypeStruct((parts, tokens + CODES, width), jnp.int16),
        ],
        scratch_shapes=[pltpu.VMEM((CODES, BLOCK), F32), pltpu.VMEM((parts, BLOCK, width), F32)],
        name="forward",
    )(gate, up, weight)


def share_kernel(coded_ref, codes_ref, target_ref, gain_ref, share_ref, stats_ref):
    step = pl.program_id(0)
    parts = coded_ref.shape[0]
    codes = codes_ref[...][:, :, :BLOCK].astype(jnp.int32).astype(F32)
    here = lax.broadcasted_iota(jnp.int32, codes.shape, 1) == step
    factors = columns_of(jnp.exp2(0.125 * jnp.sum(jnp.where(here, codes, 0.0), axis=1) - 15.0))
    share = jnp.zeros(share_ref.shape, F32)
    for part in range(parts):
        share += coded_ref[part].astype(jnp.int32).astype(F32) * factors[:, part : part + 1]
    share_ref[...] = share
    gain = gain_ref[...]
    scaled = share * gain
    square = jnp.sum(share * share, axis=1, keepdims=True)
    gained = jnp.sum(scaled * scaled, axis=1, keepdims=True)
    crossed = jnp.sum(target_ref[...].astype(F32) * scaled, axis=1, keepdims=True)
    lane = lax.broadcasted_iota(jnp.int32, (BLOCK, BLOCK), 1)
    packed = jnp.where(lane == 0, square, jnp.where(lane == 1, gained, jnp.where(lane == 2, crossed, 0.0)))
    stats = packed.T[:8, :]
    for part in range(parts):
        stats_ref[part] = stats


def share_and_stats(coded, target, gain):
    parts, _, width = coded.shape
    tokens = target.shape[0]
    return pl.pallas_call(
        share_kernel,
        grid=(tokens // BLOCK,),
        in_specs=[
            pl.BlockSpec((parts, BLOCK, width), lambda i: (0, i, 0)),
            pl.BlockSpec((parts, CODES, width), lambda i: (0, tokens // CODES, 0)),
            pl.BlockSpec((BLOCK, width), lambda i: (i, 0)),
            pl.BlockSpec((1, width), lambda i: (0, 0)),
        ],
        out_specs=[
            pl.BlockSpec((BLOCK, width), lambda i: (i, 0)),
            pl.BlockSpec((parts, 8, BLOCK), lambda i: (0, 0, i)),
        ],
        out_shape=[
            jax.ShapeDtypeStruct((tokens, width), F32),
            jax.ShapeDtypeStruct((parts, 8, tokens), F32),
        ],
        name="share",
    )(coded, coded, target, gain)


def grad_kernel(share_ref, stats_ref, target_ref, gain_ref, normed_ref, grad_ref, *copies_refs):
    stats = jnp.sum(stats_ref[...], axis=0)
    features = share_ref.shape[1] * stats_ref.shape[0]
    square, gained, crossed = stats[0:1, :], stats[1:2, :], stats[2:3, :]
    inv_rms = lax.rsqrt(square / features + EPSILON)
    inner = inv_rms * (inv_rms * gained - crossed) / features
    columns = columns_of(jnp.concatenate([inv_rms, inner, jnp.zeros((6, BLOCK), F32)], axis=0))
    inv_col, inner_col = columns[:, 0:1], columns[:, 1:2]
    gain = gain_ref[...]
    normal = share_ref[...] * inv_col
    output = normal * gain
    grad_norm = (output - target_ref[...].astype(F32)) * gain
    grad = (inv_col * (grad_norm - normal * inner_col)).astype(BF16)
    normed_ref[...] = output.astype(BF16)
    grad_ref[...] = grad
    for half, copies_ref in enumerate(copies_refs):
        width = copies_ref.shape[2]
        for part in range(copies_ref.shape[0]):
            copies_ref[part] = grad[:, half * width : (half + 1) * width]


def grads(share, stats, target, gain, pieces):
    tokens, width = share.shape
    parts = stats.shape[0]
    block = pl.BlockSpec((BLOCK, width), lambda i: (i, 0))
    copies = pl.BlockSpec((parts, BLOCK, width // max(pieces, 1)), lambda i: (0, i, 0))
    return pl.pallas_call(
        grad_kernel,
        grid=(tokens // BLOCK,),
        in_specs=[
            block,
            pl.BlockSpec((parts, 8, BLOCK), lambda i: (0, 0, i)),
            block,
            pl.BlockSpec((1, width), lambda i: (0, 0)),
        ],
        out_specs=[block, block] + [copies] * pieces,
        out_shape=[
            jax.ShapeDtypeStruct((tokens, width), BF16),
            jax.ShapeDtypeStruct((tokens, width), BF16),
        ]
        + [jax.ShapeDtypeStruct((parts, tokens, width // pieces), BF16) for _ in range(pieces)],
        name="grads",
    )(share, stats, target, gain)


def updated(rate_ref, hidden_ref, grad, weight):
    weight_grad = jnp.dot(hidden_ref[...], grad, preferred_element_type=F32)
    return (weight.astype(F32) - rate_ref[0] * weight_grad).astype(BF16)


def beside(one, other):
    return jnp.concatenate([one, other], axis=1)


def in_pairs(count, body):
    def both(number, _):
        body(2 * number)
        body(2 * number + 1)
        return 0

    lax.fori_loop(0, count // 2, both, 0)


def update_kernel(rate_ref, hidden_ref, *refs):
    *grad_refs, weight_ref, updated_ref = refs
    parts, _, width = grad_refs[0].shape

    def one_part(part):
        columns = columns_at(part, width * len(grad_refs))
        grad = grad_refs[0][part] if len(grad_refs) == 1 else beside(grad_refs[0][part], grad_refs[1][part])
        updated_ref[:, columns] = updated(rate_ref, hidden_ref, grad, weight_ref[:, columns])

    in_pairs(parts, one_part)


def half_update_kernel(half, rate_ref, hidden_ref, grad_ref, weight_ref, updated_ref):
    parts, _, width = grad_ref.shape

    def one_pair(pair):
        grad = beside(grad_ref[2 * pair], grad_ref[2 * pair + 1])
        weight = beside(*(weight_ref[:, columns_at(4 * pair + 2 * k + half, width)] for k in range(2)))
        updated_ref[:, columns_at(pair, 2 * width)] = updated(rate_ref, hidden_ref, grad, weight)

    in_pairs(parts // 2, one_pair)


def paired_update_kernel(half, rate_ref, hidden_ref, grad_ref, weight_ref, updated_ref):
    pairs, _, width = grad_ref.shape

    def one_pair(pair):
        weight = beside(*(weight_ref[:, columns_at(4 * pair + 2 * k + half, width // 2)] for k in range(2)))
        updated_ref[:, columns_at(pair, width)] = updated(rate_ref, hidden_ref, grad_ref[pair], weight)

    in_pairs(pairs, one_pair)


def update(kernel, rate, hidden_t, grads, weight, first, rows, block, width):
    tokens, features = hidden_t.shape[1], weight.shape[1]
    skip = first // block
    hidden_skip = (hidden_t.shape[0] - weight.shape[0] + first) // block
    return pl.pallas_call(
        kernel,
        grid=(rows // block,),
        in_specs=[
            pl.BlockSpec(memory_space=pltpu.SMEM),
            pl.BlockSpec((block, tokens), lambda i: (i + hidden_skip, 0)),
            *(pl.BlockSpec(memory_space=pltpu.VMEM) for _ in grads),
            pl.BlockSpec((block, features), lambda i: (i + skip, 0)),
        ],
        out_specs=pl.BlockSpec((block, width), lambda i: (i, 0)),
        out_shape=jax.ShapeDtypeStruct((rows, width), BF16),
        name="update",
    )(rate, hidden_t, *grads, weight)


def averaged(one, other):
    return (0.5 * (one.astype(F32) + other.astype(F32))).astype(BF16)


def mix_early_kernel(rate_ref, hidden_ref, grad_ref, weight_ref, own_ref, *refs):
    mixed_ref = refs[-1]
    parts, _, width = grad_ref.shape

    def one_part(part):
        columns = columns_at(part, width)
        peer = updated(rate_ref, hidden_ref, grad_ref[part], weight_ref[:, columns])
        mixed_ref[:, columns] = averaged(own_ref[:, columns], peer)

    in_pairs(parts, one_part)


def mix_early(rate, hidden_t, grad, weight, own, first, block, held, rows):
    early, tokens = hidden_t.shape
    features = weight.shape[1]
    skip = first // block
    kept = () if held is None else (held,)
    here = pl.BlockSpec((block, features), lambda i: (i, 0))
    there = pl.BlockSpec((block, features), lambda i: (i + skip, 0))
    return pl.pallas_call(
        mix_early_kernel,
        grid=(early // block,),
        in_specs=[
            pl.BlockSpec(memory_space=pltpu.SMEM),
            pl.BlockSpec((block, tokens), lambda i: (i, 0)),
            pl.BlockSpec(memory_space=pltpu.VMEM),
            here,
            there,
            *(pl.BlockSpec(memory_space=pl.ANY) for _ in kept),
        ],
        out_specs=there,
        out_shape=jax.ShapeDtypeStruct((rows, features), BF16),
        input_output_aliases={5: 0} if kept else {},
        name="mix_early",
    )(rate, hidden_t, grad, weight, own, *kept)


def mix_late_kernel(own_ref, peer_ref, *refs):
    refs[-1][...] = averaged(own_ref[...], peer_ref[...])


def mix_late(own, peer, piece, pieces, width, first, block, held, rows):
    late, features = own.shape
    kept = () if held is None else (held,)
    skip = first // block
    wide = width // pieces if pieces > 1 else features
    here = pl.BlockSpec((block, wide), lambda i, j: (i, j))
    return pl.pallas_call(
        mix_late_kernel,
        grid=(late // block, features // wide),
        in_specs=[here, here] + [pl.BlockSpec(memory_space=pl.ANY) for _ in kept],
        out_specs=pl.BlockSpec((block, wide), lambda i, j: (i + skip, pieces * j + piece)),
        out_shape=jax.ShapeDtypeStruct((rows, pieces * features), BF16),
        input_output_aliases={2: 0} if kept else {},
        name="mix_late",
    )(own, peer, *kept)


def exchanged(parts, axes=TP):
    return lax.all_to_all(parts, axes, split_axis=0, concat_axis=0, tiled=True)


def step(level, gate, up, target, gain, weight, rate):
    count = lax.axis_size("dp")
    parts = lax.axis_size(TP)
    rows, features = weight.shape
    width = features // parts
    back, straight, block, halves, paired, late_first = PLANS[level]
    early = back + straight
    by = 1 << level

    def sent(array, by):
        return lax.ppermute(array, "dp", [(i, (i + by) % count) for i in range(count)])

    def two_hops(array):
        for _ in range(2):
            array = sent(array, (by - count) // 2)
        return array

    if early:
        peer_weight = sent(weight[back:early], by)
    if back:
        peer_weight_back = two_hops(weight[:back])
    hidden_t, coded = forward(gate, up, weight, parts)
    hidden_late = hidden_t
    if early:
        peer_hidden = sent(hidden_t[back:early], by)
        hidden_late = hidden_t[early - block :]
    if back:
        hidden_back = hidden_t[:back]
        peer_hidden_back = two_hops(hidden_back)
    coded = exchanged(coded)
    share, stats = share_and_stats(coded, target, gain)
    stats = exchanged(stats)
    normed, grad_share, *copies = grads(share, stats, target, gain, 0 if paired else 1 + halves)
    if early:
        peer_share = sent(grad_share, by)
    pieces = 1 + halves
    if paired:
        pairs = lax.axis_size("tp_0")
        other = lax.ppermute(grad_share, "tp_1", [(0, 1), (1, 0)])
        first = lax.axis_index("tp_1") == 0
        piece = width // pieces
        for half in range(pieces):
            one, two = (x[:, half * piece : (half + 1) * piece] for x in (grad_share, other))
            both = jnp.concatenate([jnp.where(first, one, two), jnp.where(first, two, one)], axis=1)
            copies.append(jnp.broadcast_to(both, (pairs, *both.shape)))
    grad = []
    for half in range(pieces):
        grad.append(exchanged(copies[half], "tp_0" if paired else TP))
    rate = rate * FF ** (-0.5)
    own_late, peer_late = [], []
    for half in range(pieces):
        kernel = update_kernel
        if halves:
            kernel = functools.partial(paired_update_kernel if paired else half_update_kernel, half)
        own_late.append(
            update(
                kernel, rate, hidden_late, grad[half : half + 1], weight, early, rows - early, block,
                features // pieces,
            )
        )
        peer_late.append(sent(own_late[half], by))
    mixed = None

    def mix_pieces(mixed):
        tall = math.gcd(early, rows - early) if early else rows
        for piece in range(pieces):
            mixed = mix_late(
                own_late[piece], peer_late[piece], piece, pieces, width, early, tall, mixed, rows
            )
        return mixed

    if early:
        peer_grad = exchanged(jnp.broadcast_to(peer_share, (parts, *peer_share.shape)))
        own_early = update(update_kernel, rate, hidden_t, grad, weight, 0, early, block, features)
    if late_first:
        mixed = mix_pieces(mixed)
    if back:
        mixed = mix_early(
            rate, peer_hidden_back, peer_grad, peer_weight_back, own_early, 0, block, mixed, rows
        )
    if early:
        mixed = mix_early(rate, peer_hidden, peer_grad, peer_weight, own_early, back, block, mixed, rows)
    if not late_first:
        mixed = mix_pieces(mixed)
    return normed, mixed


def shards(gate_pre, up_pre, target, norm_gain, weight, round_index):
    rate = step_rate(round_index).reshape(1)
    levels = lax.axis_size("dp").bit_length() - 1
    level = round_index[0] % levels
    branches = [functools.partial(step, number) for number in range(levels)]
    normed, mixed = lax.switch(level, branches, gate_pre, up_pre, target, norm_gain[None], weight[0], rate)
    return normed, mixed[None]


def solution(mesh):
    finer = Mesh(mesh.devices.reshape(mesh.shape["dp"], 4, 2), ("dp", "tp_0", "tp_1"))
    placed = (P("dp", TP), P("dp", TP), P("dp", TP), P(TP), P("dp", TP, None), P())
    return jax.shard_map(
        shards,
        mesh=finer,
        in_specs=placed,
        out_specs=(P("dp", TP), P("dp", TP, None)),
        check_vma=False,
    )
```

profile of v0, /device:TPU:1, one launch (start us, length us, event | category | flops | bytes accessed | tf_op | source)
XLA Modules:
  0.0 217.9 jit_solution(11983016746260861102)
XLA Ops:
  1.3 216.4 %conditional.1 = (bf16[768,256]{1,0:T(8,128)(2,1)}, bf16[1,896,2048]{2,1,0:T(8,128)(2,1)}) conditional(s32[]{:T(128)} %clamp.3, (bf16[768,896]{1,0:T(8,128)(2,1)}, bf16[768,896]{1,0:T(8,128)(2,1)}, bf16[1,896,2048]{2,1,0:T(8,128)(2,1)}, bf16[768,256]{1,0:T(8,128)(2,1)}, f32[256]{0:T(256)}, /*index=5*/f32[]{:T(128)}, (), ...), branch_computations={%region_0.1_spmd, %region_1.2_spmd, %region_2.3_spmd, %region_3.4_... | conditional | flops 1966087 | bytes 90264200 | solution.py:425
  1.3 12.5 %forward.7 = (bf16[896,768]{1,0:T(8,128)(2,1)}, s16[8,784,256]{2,1,0:T(8,128)(2,1)}) custom-call(bf16[768,896]{1,0:T(8,128)(2,1)} %get-tuple-element.160.gate_ref, bf16[768,896]{1,0:T(8,128)(2,1)} %get-tuple-element.165.up_ref, bf16[896,2048]{1,0:T(8,128)(2,1)} %bitcast.36), custom_call_target="tpu_custom_call" | custom-call | tf_op jit(solution)/shard_map/cond/branch_2_fun/forward/pallas_call | solution.py:85
  13.8 0.0 copy-start.2
  13.8 0.0 copy-start.24
  13.8 46.9 %all_to_all.88.coded_ref.codes_ref = s16[8,784,256]{2,1,0:T(8,128)(2,1)} all-to-all(s16[8,784,256]{2,1,0:T(8,128)(2,1)} %get-tuple-element.88), channel_id=1, replica_groups=mesh['dp'=32,'tp_0'=4,'tp_1'=2] {'tp_0','tp_1'}, dimensions={0} | all-to-all | bytes 6422528 | tf_op jit(solution)/shard_map/cond/branch_2_fun/all_to_all | solution.py:330
  60.7 0.0 copy-done.2
  60.7 0.0 copy-done.24
  60.7 6.0 %share.7 = (f32[768,256]{1,0:T(8,128)}, f32[8,8,768]{2,1,0:T(8,128)}) custom-call(s16[8,784,256]{2,1,0:T(8,128)(2,1)} %all_to_all.88.coded_ref.codes_ref, s16[8,784,256]{2,1,0:T(8,128)(2,1)} %all_to_all.88.coded_ref.codes_ref, bf16[768,256]{1,0:T(8,128)(2,1)S(1)} %copy-done.2, f32[1,256]{1,0:T(1,128)S(1)} %bitcast.55), custom_call_target="tpu_custom_call" | custom-call | tf_op jit(solution)/shard_map/cond/branch_2_fun/share/pallas_call | solution.py:131
  66.7 11.3 %all_to_all.89.stats_ref = f32[8,8,768]{2,1,0:T(8,128)} all-to-all(f32[8,8,768]{2,1,0:T(8,128)} %get-tuple-element.92), channel_id=1, replica_groups=mesh['dp'=32,'tp_0'=4,'tp_1'=2] {'tp_0','tp_1'}, dimensions={0} | all-to-all | bytes 393216 | tf_op jit(solution)/shard_map/cond/branch_2_fun/all_to_all | solution.py:330
  78.1 5.4 %grads.7 = (bf16[768,256]{1,0:T(8,128)(2,1)}, bf16[768,256]{1,0:T(8,128)(2,1)}, bf16[8,768,256]{2,1,0:T(8,128)(2,1)}) custom-call(f32[768,256]{1,0:T(8,128)} %get-tuple-element.91.share_ref, f32[8,8,768]{2,1,0:T(8,128)} %all_to_all.89.stats_ref, bf16[768,256]{1,0:T(8,128)(2,1)S(1)} %copy-done.2, f32[1,256]{1,0:T(1,128)S(1)} %bitcast.56), custom_call_target="tpu_custom_call" | custom-call | tf_op jit(solution)/shard_map/cond/branch_2_fun/grads/pallas_call | solution.py:178
  83.4 3.9 %all-to-all-start.11 = ((bf16[8,768,256]{2,1,0:T(8,128)(2,1)}), bf16[8,768,256]{2,1,0:T(8,128)(2,1)S(1)}, u32[]{:S(2)}, u32[]{:S(2)}) async-start(bf16[8,768,256]{2,1,0:T(8,128)(2,1)} %get-tuple-element.97), calls=%async_computation.11 | async-start | bytes 6291456 | tf_op jit(solution)/shard_map/cond/branch_2_fun/all_to_all | solution.py:330
  87.3 1.7 collective-permute-start.7
  89.1 3.7 %slice_bitcast_fusion = bf16[672,2048]{1,0:T(8,128)(2,1)} fusion(bf16[1,896,2048]{2,1,0:T(8,128)(2,1)} %get-tuple-element.195), kind=kLoop, calls=%fused_computation.12 | loop fusion | bytes 5505024 | tf_op jit(solution)/shard_map/cond/branch_2_fun/slice | solution.py:351
  92.8 1.8 collective-permute-start.8
  94.5 4.8 %collective-permute-done.7 = bf16[768,256]{1,0:T(8,128)(2,1)S(1)} collective-permute-done((bf16[768,256]{1,0:T(8,128)(2,1)}, bf16[768,256]{1,0:T(8,128)(2,1)S(1)}, u32[]{:S(2)}, u32[]{:S(2)}) %collective-permute-start.7) | collective-permute-done | bytes 393248 | tf_op jit(solution)/shard_map/cond/branch_2_fun/ppermute | solution.py:343
  99.4 24.1 %all-to-all-done.11.refs_0_ = bf16[8,768,256]{2,1,0:T(8,128)(2,1)S(1)} async-done(((bf16[8,768,256]{2,1,0:T(8,128)(2,1)}), bf16[8,768,256]{2,1,0:T(8,128)(2,1)S(1)}, u32[]{:S(2)}, u32[]{:S(2)}) %all-to-all-start.11) | async-done | bytes 3145760 | tf_op jit(solution)/shard_map/cond/branch_2_fun/all_to_all | solution.py:330
  123.4 0.0 copy-start.6
  123.4 2.0 broadcast_in_dim.33
  125.5 0.7 copy-done.6
  126.1 6.2 %all-to-all-start.10 = ((bf16[8,768,256]{2,1,0:T(8,128)(2,1)}), bf16[8,768,256]{2,1,0:T(8,128)(2,1)}, u32[]{:S(2)}, u32[]{:S(2)}) async-start(bf16[8,768,256]{2,1,0:T(8,128)(2,1)} %broadcast_in_dim.33), calls=%async_computation.10 | async-start | bytes 6291456 | tf_op jit(solution)/shard_map/cond/branch_2_fun/all_to_all | solution.py:330
  132.3 1.3 slice.46
  133.6 1.7 collective-permute-start.6
  135.3 2.0 slice.48.hidden_ref
  137.4 4.6 %update.16.own_ref = bf16[224,2048]{1,0:T(8,128)(2,1)} custom-call(f32[1]{0:T(128)} %bitcast.10.rate_ref, bf16[448,768]{1,0:T(8,128)(2,1)} %slice.48.hidden_ref, bf16[8,768,256]{2,1,0:T(8,128)(2,1)} %copy-done.6, bf16[896,2048]{1,0:T(8,128)(2,1)} %bitcast.37), custom_call_target="tpu_custom_call" | custom-call | tf_op jit(solution)/shard_map/cond/branch_2_fun/update/pallas_call | solution.py:252
  142.0 1.8 collective-permute-start.9
  143.8 7.9 %update.15.own_ref = bf16[672,2048]{1,0:T(8,128)(2,1)} custom-call(f32[1]{0:T(128)} %bitcast.10.rate_ref, bf16[896,768]{1,0:T(8,128)(2,1)} %get-tuple-element.95.hidden_ref, bf16[8,768,256]{2,1,0:T(8,128)(2,1)} %copy-done.6, bf16[896,2048]{1,0:T(8,128)(2,1)} %bitcast.38), custom_call_target="tpu_custom_call" | custom-call | tf_op jit(solution)/shard_map/cond/branch_2_fun/update/pallas_call | solution.py:252
  151.7 48.5 %collective-permute-done.9.peer_ref = bf16[224,2048]{1,0:T(8,128)(2,1)S(1)} collective-permute-done((bf16[224,2048]{1,0:T(8,128)(2,1)}, bf16[224,2048]{1,0:T(8,128)(2,1)S(1)}, u32[]{:S(2)}, u32[]{:S(2)}) %collective-permute-start.9) | collective-permute-done | bytes 917536 | tf_op jit(solution)/shard_map/cond/branch_2_fun/ppermute | solution.py:343
  200.2 0.0 copy-start.18
  200.2 0.9 copy-done.18
  201.1 2.6 %mix_late.12.refs_0_ = bf16[896,2048]{1,0:T(8,128)(2,1)} custom-call(bf16[224,2048]{1,0:T(8,128)(2,1)} %update.16.own_ref, bf16[224,2048]{1,0:T(8,128)(2,1)} %copy-done.18), custom_call_target="tpu_custom_call" | custom-call | tf_op jit(solution)/shard_map/cond/branch_2_fun/mix_late/pallas_call | solution.py:318
  203.7 0.0 collective-permute-done.6.hidden_ref
  203.7 0.0 copy-start.17
  203.7 0.0 collective-permute-done.8.weight_ref
  203.7 0.0 all-to-all-done.10.grad_ref
  203.8 1.0 copy-done.17
  204.7 9.1 %mix_early.4 = bf16[896,2048]{1,0:T(8,128)(2,1)} custom-call(f32[1]{0:T(128)} %bitcast.10.rate_ref, bf16[672,768]{1,0:T(8,128)(2,1)} %copy-done.17, bf16[8,768,256]{2,1,0:T(8,128)(2,1)} %all-to-all-done.10.grad_ref, bf16[672,2048]{1,0:T(8,128)(2,1)} %collective-permute-done.8.weight_ref, ...), custom_call_target="tpu_custom_call", output_to_operand_aliasing={{}: (5, {})} | custom-call | tf_op jit(solution)/shard_map/cond/branch_2_fun/mix_early/pallas_call | solution.py:290
Async XLA Ops:
  13.8 46.9 %copy-start.2 = (bf16[768,256]{1,0:T(8,128)(2,1)S(1)}, bf16[768,256]{1,0:T(8,128)(2,1)}, u32[]{:S(2)}) copy-start(bf16[768,256]{1,0:T(8,128)(2,1)} %get-tuple-element.175.target_ref) | copy-start | bytes 1179652 | tf_op jit(solution)/shard_map/cond
  13.8 46.9 %copy-start.24 = (f32[256]{0:T(256)S(1)}, f32[256]{0:T(256)}, u32[]{:S(2)}) copy-start(f32[256]{0:T(256)} %get-tuple-element.200) | copy-start | bytes 3076 | tf_op jit(solution)/shard_map/cond
  83.4 40.0 %all-to-all-start.11 = ((bf16[8,768,256]{2,1,0:T(8,128)(2,1)}), bf16[8,768,256]{2,1,0:T(8,128)(2,1)S(1)}, u32[]{:S(2)}, u32[]{:S(2)}) async-start(bf16[8,768,256]{2,1,0:T(8,128)(2,1)} %get-tuple-element.97), calls=%async_computation.11 | async-start | bytes 6291456 | tf_op jit(solution)/shard_map/cond/branch_2_fun/all_to_all | solution.py:330
  87.3 12.0 %collective-permute-start.7 = (bf16[768,256]{1,0:T(8,128)(2,1)}, bf16[768,256]{1,0:T(8,128)(2,1)S(1)}, u32[]{:S(2)}, u32[]{:S(2)}) collective-permute-start(bf16[768,256]{1,0:T(8,128)(2,1)} %get-tuple-element.96), channel_id=1, source_target_pairs={{0,32},{8,40},{16,48},{24,56},{32,64},{40,72},{48,80},{56,88},{64,... | collective-permute-start | bytes 1179656 | tf_op jit(solution)/shard_map/cond/branch_2_fun/ppermute | solution.py:343
  92.8 111.0 %collective-permute-start.8 = (bf16[672,2048]{1,0:T(8,128)(2,1)}, bf16[672,2048]{1,0:T(8,128)(2,1)}, u32[]{:S(2)}, u32[]{:S(2)}) collective-permute-start(bf16[672,2048]{1,0:T(8,128)(2,1)} %slice_bitcast_fusion), channel_id=1, source_target_pairs={{0,32},{8,40},{16,48},{24,56},{32,64},{40,72},{48,80},{56,88},{64,... | collective-permute-start | bytes 8257544 | tf_op jit(solution)/shard_map/cond/branch_2_fun/ppermute | solution.py:343
  123.4 2.7 %copy-start.6 = (bf16[8,768,256]{2,1,0:T(8,128)(2,1)}, bf16[8,768,256]{2,1,0:T(8,128)(2,1)S(1)}, u32[]{:S(2)}) copy-start(bf16[8,768,256]{2,1,0:T(8,128)(2,1)S(1)} %all-to-all-done.11.refs_0_) | copy-start | bytes 9437188 | tf_op jit(solution)/shard_map/cond
  126.1 77.6 %all-to-all-start.10 = ((bf16[8,768,256]{2,1,0:T(8,128)(2,1)}), bf16[8,768,256]{2,1,0:T(8,128)(2,1)}, u32[]{:S(2)}, u32[]{:S(2)}) async-start(bf16[8,768,256]{2,1,0:T(8,128)(2,1)} %broadcast_in_dim.33), calls=%async_computation.10 | async-start | bytes 6291456 | tf_op jit(solution)/shard_map/cond/branch_2_fun/all_to_all | solution.py:330
  133.6 70.1 %collective-permute-start.6 = (bf16[672,768]{1,0:T(8,128)(2,1)S(1)}, bf16[672,768]{1,0:T(8,128)(2,1)S(1)}, u32[]{:S(2)}, u32[]{:S(2)}) collective-permute-start(bf16[672,768]{1,0:T(8,128)(2,1)S(1)} %slice.46), channel_id=1, source_target_pairs={{0,32},{8,40},{16,48},{24,56},{32,64},{40,72},{48,80},{56,88},{64,... | collective-permute-start | bytes 3096584 | tf_op jit(solution)/shard_map/cond/branch_2_fun/ppermute | solution.py:343
  142.0 58.1 %collective-permute-start.9 = (bf16[224,2048]{1,0:T(8,128)(2,1)}, bf16[224,2048]{1,0:T(8,128)(2,1)S(1)}, u32[]{:S(2)}, u32[]{:S(2)}) collective-permute-start(bf16[224,2048]{1,0:T(8,128)(2,1)} %update.16.own_ref), channel_id=1, source_target_pairs={{0,32},{8,40},{16,48},{24,56},{32,64},{40,72},{48,80},{56,88},{64,... | collective-permute-start | bytes 2752520 | tf_op jit(solution)/shard_map/cond/branch_2_fun/ppermute | solution.py:343
  200.2 0.9 copy-start.18
  203.7 1.0 copy-start.17
where the time goes:
time: 222 us; the launch traced here: 218 us
  waiting for transfers between devices  77.4 us (35%)
  blocking collectives  58.2 us (26%)
  Pallas kernels  48 us (22%)
  starting transfers between devices  17 us (8%)
  local copies, waits for them, and re-layouts  11.6 us (5%)
  loops' own time  4.11 us (2%)
    all_to_all x2, blocking collectives, exchanged(): return lax.all_to_all(parts, axes, split_axis=0, concat_axis=0, tiled=True)  58.2 us
    ppermute x4, waiting for transfers between devices, sent(): lax.ppermute(array, 'dp', [(i, (i + by) % count) for i in range(count)])  53.3 us
    all_to_all x2, waiting for transfers between devices, exchanged(): return lax.all_to_all(parts, axes, split_axis=0, concat_axis=0, tiled=True)  24.1 us
    pallas_call x2, Pallas kernels, update(): pl.pallas_call(kernel, grid=(rows // block,), in_specs=[pl.BlockSpec(memo...  12.5 us
    pallas_call x1, Pallas kernels, forward(): pl.pallas_call(forward_kernel, grid=(tokens // BLOCK,), in_specs=[pl.Bloc...  12.5 us
    all_to_all x2, starting transfers between devices, exchanged(): return lax.all_to_all(parts, axes, split_axis=0, concat_axis=0, tiled=True)  10.1 us
    pallas_call x1, Pallas kernels, mix_early(): pl.pallas_call(mix_early_kernel, grid=(early // block,), in_specs=[pl.Blo...  9.06 us
    ppermute x4, starting transfers between devices, sent(): lax.ppermute(array, 'dp', [(i, (i + by) % count) for i in range(count)])  6.98 us
  transfers between devices with their start and end apart: 6, of which 3 were waited for; matrix products, arithmetic and copies ran while one was open for 4% of the time, Pallas kernels for 7%

commit v1 on v0

--- a/solution.py
+++ b/solution.py
@@ -22,7 +22,7 @@
     (0, 0, 224, True, True, False),
     (0, 672, 224, False, False, True),
     (224, 336, 112, False, False, False),
-    (0, 448, 224, True, False, False),
+    (0, 384, 128, True, False, False),
 )
 
 
@@ -47,18 +47,10 @@
     hidden = hidden.astype(BF16)
     parts, _, width = coded_ref.shape
 
-    def products(number, top):
-        weight = weight_ref[:, columns_at(number, 4 * width)]
-        partial = jnp.dot(hidden, weight, preferred_element_type=F32) * FF ** (-0.5)
-        for part in range(4):
-            values = partial[:, part * width : (part + 1) * width]
-            partial_scr[4 * number + part] = values
-            for lanes in range(0, width, BLOCK):
-                top = jnp.maximum(top, jnp.abs(values[:, lanes : lanes + BLOCK]))
-        return top
-
-    top = lax.fori_loop(0, parts // 4, products, jnp.zeros((BLOCK, BLOCK), F32))
-    top = jnp.max(top, axis=1, keepdims=True)
+    partial = jnp.dot(hidden, weight_ref[...], preferred_element_type=F32) * FF ** (-0.5)
+    top = jnp.max(jnp.abs(partial), axis=1, keepdims=True)
+    for part in range(parts):
+        partial_scr[part] = partial[:, part * width : (part + 1) * width]
     level = jnp.ceil(8.0 * jnp.log2(jnp.maximum(top, 1e-30))) + 1.0
     factor = jnp.exp2(15.0 - 0.125 * level)
     rows = pl.ds(pl.multiple_of(step * BLOCK, BLOCK), BLOCK)
@@ -305,25 +297,35 @@
     )(rate, hidden_t, grad, weight, own, *kept)
 
 
-def mix_late_kernel(own_ref, peer_ref, *refs):
-    refs[-1][...] = averaged(own_ref[...], peer_ref[...])
-
-
-def mix_late(own, peer, piece, pieces, width, first, block, held, rows):
-    late, features = own.shape
+def mix_late_kernel(pieces, width, *refs):
+    own_refs, peer_refs, mixed_ref = refs[:pieces], refs[pieces : 2 * pieces], refs[-1]
+
+    def one_part(part, _):
+        columns = columns_at(part, width)
+        for piece in range(pieces):
+            mixed_ref[:, columns_at(part * pieces + piece, width)] = averaged(
+                own_refs[piece][:, columns], peer_refs[piece][:, columns]
+            )
+        return 0
+
+    lax.fori_loop(0, own_refs[0].shape[1] // width, one_part, 0)
+
+
+def mix_late(own, peer, width, first, block, held, rows):
+    late, features = own[0].shape
+    pieces = len(own)
     kept = () if held is None else (held,)
     skip = first // block
-    wide = width // pieces if pieces > 1 else features
-    here = pl.BlockSpec((block, wide), lambda i, j: (i, j))
-    return pl.pallas_call(
-        mix_late_kernel,
-        grid=(late // block, features // wide),
-        in_specs=[here, here] + [pl.BlockSpec(memory_space=pl.ANY) for _ in kept],
-        out_specs=pl.BlockSpec((block, wide), lambda i, j: (i + skip, pieces * j + piece)),
+    here = pl.BlockSpec((block, features), lambda i: (i, 0))
+    return pl.pallas_call(
+        functools.partial(mix_late_kernel, pieces, width // pieces),
+        grid=(late // block,),
+        in_specs=[here] * (2 * pieces) + [pl.BlockSpec(memory_space=pl.ANY) for _ in kept],
+        out_specs=pl.BlockSpec((block, pieces * features), lambda i: (i + skip, 0)),
         out_shape=jax.ShapeDtypeStruct((rows, pieces * features), BF16),
-        input_output_aliases={2: 0} if kept else {},
+        input_output_aliases={2 * pieces: 0} if kept else {},
         name="mix_late",
-    )(own, peer, *kept)
+    )(*own, *peer, *kept)
 
 
 def exchanged(parts, axes=TP):
@@ -350,7 +352,8 @@
     if early:
         peer_weight = sent(weight[back:early], by)
     if back:
-        peer_weight_back = two_hops(weight[:back])
+        weight_back = weight[:back]
+        peer_weight_back = two_hops(weight_back)
     hidden_t, coded = forward(gate, up, weight, parts)
     hidden_late = hidden_t
     if early:
@@ -394,24 +397,19 @@
     mixed = None
 
     def mix_pieces(mixed):
-        tall = math.gcd(early, rows - early) if early else rows
-        for piece in range(pieces):
-            mixed = mix_late(
-                own_late[piece], peer_late[piece], piece, pieces, width, early, tall, mixed, rows
-            )
-        return mixed
+        return mix_late(own_late, peer_late, width, early, block, mixed, rows)
 
     if early:
         peer_grad = exchanged(jnp.broadcast_to(peer_share, (parts, *peer_share.shape)))
         own_early = update(update_kernel, rate, hidden_t, grad, weight, 0, early, block, features)
     if late_first:
         mixed = mix_pieces(mixed)
+    if early:
+        mixed = mix_early(rate, peer_hidden, peer_grad, peer_weight, own_early, back, block, mixed, rows)
     if back:
         mixed = mix_early(
             rate, peer_hidden_back, peer_grad, peer_weight_back, own_early, 0, block, mixed, rows
         )
-    if early:
-        mixed = mix_early(rate, peer_hidden, peer_grad, peer_weight, own_early, back, block, mixed, rows)
     if not late_first:
         mixed = mix_pieces(mixed)
     return normed, mixed

time: 222 us -> 220 us (level)
  no operation moved by 1% of the time
where the time goes in v1:
time: 220 us; the launch traced here: 216 us
  waiting for transfers between devices  77.8 us (35%)
  blocking collectives  58.5 us (27%)
  Pallas kernels  46.2 us (21%)
  starting transfers between devices  16.4 us (7%)
  local copies, waits for them, and re-layouts  11.6 us (5%)
  loops' own time  4.05 us (2%)
    all_to_all x2, blocking collectives, exchanged(): return lax.all_to_all(parts, axes, split_axis=0, concat_axis=0, tiled=True)  58.5 us
    ppermute x4, waiting for transfers between devices, sent(): lax.ppermute(array, 'dp', [(i, (i + by) % count) for i in range(count)])  53.4 us
    all_to_all x2, waiting for transfers between devices, exchanged(): return lax.all_to_all(parts, axes, split_axis=0, concat_axis=0, tiled=True)  24.3 us
    pallas_call x2, Pallas kernels, update(): pl.pallas_call(kernel, grid=(rows // block,), in_specs=[pl.BlockSpec(memo...  12.5 us
    pallas_call x1, Pallas kernels, forward(): pl.pallas_call(forward_kernel, grid=(tokens // BLOCK,), in_specs=[pl.Bloc...  10.6 us
    all_to_all x2, starting transfers between devices, exchanged(): return lax.all_to_all(parts, axes, split_axis=0, concat_axis=0, tiled=True)  9.78 us
    pallas_call x1, Pallas kernels, mix_early(): pl.pallas_call(mix_early_kernel, grid=(early // block,), in_specs=[pl.Blo...  9.06 us
    ppermute x4, starting transfers between devices, sent(): lax.ppermute(array, 'dp', [(i, (i + by) % count) for i in range(count)])  6.63 us
  transfers between devices with their start and end apart: 6, of which 3 were waited for; matrix products, arithmetic and copies ran while one was open for 4% of the time, Pallas kernels for 7%

profile of v1, /device:TPU:1, one launch (start us, length us, event | category | flops | bytes accessed | tf_op | source)
XLA Modules:
  0.0 216.1 jit_solution(13662534682577958971)
XLA Ops:
  1.3 214.6 %conditional.1 = (bf16[768,256]{1,0:T(8,128)(2,1)}, bf16[1,896,2048]{2,1,0:T(8,128)(2,1)}) conditional(s32[]{:T(128)} %clamp.3, (bf16[768,896]{1,0:T(8,128)(2,1)}, bf16[768,896]{1,0:T(8,128)(2,1)}, bf16[1,896,2048]{2,1,0:T(8,128)(2,1)}, bf16[768,256]{1,0:T(8,128)(2,1)}, f32[256]{0:T(256)}, /*index=5*/f32[]{:T(128)}, (), ...), branch_computations={%region_0.1_spmd, %region_1.2_spmd, %region_2.3_spmd, %region_3.4_... | conditional | flops 1966087 | bytes 90264208 | solution.py:423
  1.3 10.6 %forward.7 = (bf16[896,768]{1,0:T(8,128)(2,1)}, s16[8,784,256]{2,1,0:T(8,128)(2,1)}) custom-call(bf16[768,896]{1,0:T(8,128)(2,1)} %get-tuple-element.160.gate_ref, bf16[768,896]{1,0:T(8,128)(2,1)} %get-tuple-element.165.up_ref, bf16[896,2048]{1,0:T(8,128)(2,1)} %bitcast.36), custom_call_target="tpu_custom_call" | custom-call | tf_op jit(solution)/shard_map/cond/branch_2_fun/forward/pallas_call | solution.py:77
  11.9 0.0 copy-start.2
  11.9 0.0 copy-start.24
  11.9 47.0 %all_to_all.88.coded_ref.codes_ref = s16[8,784,256]{2,1,0:T(8,128)(2,1)} all-to-all(s16[8,784,256]{2,1,0:T(8,128)(2,1)} %get-tuple-element.88), channel_id=1, replica_groups=mesh['dp'=32,'tp_0'=4,'tp_1'=2] {'tp_0','tp_1'}, dimensions={0} | all-to-all | bytes 6422528 | tf_op jit(solution)/shard_map/cond/branch_2_fun/all_to_all | solution.py:332
  58.9 0.0 copy-done.2
  58.9 0.0 copy-done.24
  58.9 6.0 %share.7 = (f32[768,256]{1,0:T(8,128)}, f32[8,8,768]{2,1,0:T(8,128)}) custom-call(s16[8,784,256]{2,1,0:T(8,128)(2,1)} %all_to_all.88.coded_ref.codes_ref, s16[8,784,256]{2,1,0:T(8,128)(2,1)} %all_to_all.88.coded_ref.codes_ref, bf16[768,256]{1,0:T(8,128)(2,1)S(1)} %copy-done.2, f32[1,256]{1,0:T(1,128)S(1)} %bitcast.55), custom_call_target="tpu_custom_call" | custom-call | tf_op jit(solution)/shard_map/cond/branch_2_fun/share/pallas_call | solution.py:123
  64.9 11.6 %all_to_all.89.stats_ref = f32[8,8,768]{2,1,0:T(8,128)} all-to-all(f32[8,8,768]{2,1,0:T(8,128)} %get-tuple-element.92), channel_id=1, replica_groups=mesh['dp'=32,'tp_0'=4,'tp_1'=2] {'tp_0','tp_1'}, dimensions={0} | all-to-all | bytes 393216 | tf_op jit(solution)/shard_map/cond/branch_2_fun/all_to_all | solution.py:332
  76.5 5.4 %grads.7 = (bf16[768,256]{1,0:T(8,128)(2,1)}, bf16[768,256]{1,0:T(8,128)(2,1)}, bf16[8,768,256]{2,1,0:T(8,128)(2,1)}) custom-call(f32[768,256]{1,0:T(8,128)} %get-tuple-element.91.share_ref, f32[8,8,768]{2,1,0:T(8,128)} %all_to_all.89.stats_ref, bf16[768,256]{1,0:T(8,128)(2,1)S(1)} %copy-done.2, f32[1,256]{1,0:T(1,128)S(1)} %bitcast.56), custom_call_target="tpu_custom_call" | custom-call | tf_op jit(solution)/shard_map/cond/branch_2_fun/grads/pallas_call | solution.py:170
  81.9 3.7 %all-to-all-start.11 = ((bf16[8,768,256]{2,1,0:T(8,128)(2,1)}), bf16[8,768,256]{2,1,0:T(8,128)(2,1)S(1)}, u32[]{:S(2)}, u32[]{:S(2)}) async-start(bf16[8,768,256]{2,1,0:T(8,128)(2,1)} %get-tuple-element.97), calls=%async_computation.11 | async-start | bytes 6291456 | tf_op jit(solution)/shard_map/cond/branch_2_fun/all_to_all | solution.py:332
  85.5 1.7 collective-permute-start.7
  87.2 3.7 %slice_bitcast_fusion = bf16[672,2048]{1,0:T(8,128)(2,1)} fusion(bf16[1,896,2048]{2,1,0:T(8,128)(2,1)} %get-tuple-element.195), kind=kLoop, calls=%fused_computation.12 | loop fusion | bytes 5505024 | tf_op jit(solution)/shard_map/cond/branch_2_fun/slice | solution.py:353
  90.9 1.6 collective-permute-start.8
  92.5 5.0 %collective-permute-done.7 = bf16[768,256]{1,0:T(8,128)(2,1)S(1)} collective-permute-done((bf16[768,256]{1,0:T(8,128)(2,1)}, bf16[768,256]{1,0:T(8,128)(2,1)S(1)}, u32[]{:S(2)}, u32[]{:S(2)}) %collective-permute-start.7) | collective-permute-done | bytes 393248 | tf_op jit(solution)/shard_map/cond/branch_2_fun/ppermute | solution.py:345
  97.5 24.3 %all-to-all-done.11.refs_0_ = bf16[8,768,256]{2,1,0:T(8,128)(2,1)S(1)} async-done(((bf16[8,768,256]{2,1,0:T(8,128)(2,1)}), bf16[8,768,256]{2,1,0:T(8,128)(2,1)S(1)}, u32[]{:S(2)}, u32[]{:S(2)}) %all-to-all-start.11) | async-done | bytes 3145760 | tf_op jit(solution)/shard_map/cond/branch_2_fun/all_to_all | solution.py:332
  121.9 0.0 copy-start.6
  121.9 2.0 broadcast_in_dim.33
  123.9 0.7 copy-done.6
  124.6 6.1 %all-to-all-start.10 = ((bf16[8,768,256]{2,1,0:T(8,128)(2,1)}), bf16[8,768,256]{2,1,0:T(8,128)(2,1)}, u32[]{:S(2)}, u32[]{:S(2)}) async-start(bf16[8,768,256]{2,1,0:T(8,128)(2,1)} %broadcast_in_dim.33), calls=%async_computation.10 | async-start | bytes 6291456 | tf_op jit(solution)/shard_map/cond/branch_2_fun/all_to_all | solution.py:332
  130.7 1.3 slice.46
  132.0 1.7 collective-permute-start.6
  133.7 2.0 slice.48.hidden_ref
  135.8 4.6 %update.16.refs_0_ = bf16[224,2048]{1,0:T(8,128)(2,1)} custom-call(f32[1]{0:T(128)} %bitcast.10.rate_ref, bf16[448,768]{1,0:T(8,128)(2,1)} %slice.48.hidden_ref, bf16[8,768,256]{2,1,0:T(8,128)(2,1)} %copy-done.6, bf16[896,2048]{1,0:T(8,128)(2,1)} %bitcast.37), custom_call_target="tpu_custom_call" | custom-call | tf_op jit(solution)/shard_map/cond/branch_2_fun/update/pallas_call | solution.py:244
  140.4 1.6 collective-permute-start.9
  142.0 7.9 %update.15.own_ref = bf16[672,2048]{1,0:T(8,128)(2,1)} custom-call(f32[1]{0:T(128)} %bitcast.10.rate_ref, bf16[896,768]{1,0:T(8,128)(2,1)} %get-tuple-element.95.hidden_ref, bf16[8,768,256]{2,1,0:T(8,128)(2,1)} %copy-done.6, bf16[896,2048]{1,0:T(8,128)(2,1)} %bitcast.38), custom_call_target="tpu_custom_call" | custom-call | tf_op jit(solution)/shard_map/cond/branch_2_fun/update/pallas_call | solution.py:244
  149.9 48.4 %collective-permute-done.9.refs_1_ = bf16[224,2048]{1,0:T(8,128)(2,1)S(1)} collective-permute-done((bf16[224,2048]{1,0:T(8,128)(2,1)}, bf16[224,2048]{1,0:T(8,128)(2,1)S(1)}, u32[]{:S(2)}, u32[]{:S(2)}) %collective-permute-start.9) | collective-permute-done | bytes 917536 | tf_op jit(solution)/shard_map/cond/branch_2_fun/ppermute | solution.py:345
  198.3 0.0 copy-start.18
  198.3 0.9 copy-done.18
  199.2 2.7 %mix_late.7.refs_0_ = bf16[896,2048]{1,0:T(8,128)(2,1)} custom-call(bf16[224,2048]{1,0:T(8,128)(2,1)} %update.16.refs_0_, bf16[224,2048]{1,0:T(8,128)(2,1)} %copy-done.18), custom_call_target="tpu_custom_call" | custom-call | tf_op jit(solution)/shard_map/cond/branch_2_fun/mix_late/pallas_call | solution.py:320
  202.0 0.0 collective-permute-done.6.hidden_ref
  202.0 0.0 copy-start.17
  202.0 0.0 collective-permute-done.8.weight_ref
  202.0 0.0 all-to-all-done.10.grad_ref
  202.0 1.0 copy-done.17
  202.9 9.1 %mix_early.4 = bf16[896,2048]{1,0:T(8,128)(2,1)} custom-call(f32[1]{0:T(128)} %bitcast.10.rate_ref, bf16[672,768]{1,0:T(8,128)(2,1)} %copy-done.17, bf16[8,768,256]{2,1,0:T(8,128)(2,1)} %all-to-all-done.10.grad_ref, bf16[672,2048]{1,0:T(8,128)(2,1)} %collective-permute-done.8.weight_ref, ...), custom_call_target="tpu_custom_call", output_to_operand_aliasing={{}: (5, {})} | custom-call | tf_op jit(solution)/shard_map/cond/branch_2_fun/mix_early/pallas_call | solution.py:282
Async XLA Ops:
  11.9 47.0 %copy-start.2 = (bf16[768,256]{1,0:T(8,128)(2,1)S(1)}, bf16[768,256]{1,0:T(8,128)(2,1)}, u32[]{:S(2)}) copy-start(bf16[768,256]{1,0:T(8,128)(2,1)} %get-tuple-element.175.target_ref) | copy-start | bytes 1179652 | tf_op jit(solution)/shard_map/cond
  11.9 47.0 %copy-start.24 = (f32[256]{0:T(256)S(1)}, f32[256]{0:T(256)}, u32[]{:S(2)}) copy-start(f32[256]{0:T(256)} %get-tuple-element.200) | copy-start | bytes 3076 | tf_op jit(solution)/shard_map/cond
  81.9 40.0 %all-to-all-start.11 = ((bf16[8,768,256]{2,1,0:T(8,128)(2,1)}), bf16[8,768,256]{2,1,0:T(8,128)(2,1)S(1)}, u32[]{:S(2)}, u32[]{:S(2)}) async-start(bf16[8,768,256]{2,1,0:T(8,128)(2,1)} %get-tuple-element.97), calls=%async_computation.11 | async-start | bytes 6291456 | tf_op jit(solution)/shard_map/cond/branch_2_fun/all_to_all | solution.py:332
  85.5 12.0 %collective-permute-start.7 = (bf16[768,256]{1,0:T(8,128)(2,1)}, bf16[768,256]{1,0:T(8,128)(2,1)S(1)}, u32[]{:S(2)}, u32[]{:S(2)}) collective-permute-start(bf16[768,256]{1,0:T(8,128)(2,1)} %get-tuple-element.96), channel_id=1, source_target_pairs={{0,32},{8,40},{16,48},{24,56},{32,64},{40,72},{48,80},{56,88},{64,... | collective-permute-start | bytes 1179656 | tf_op jit(solution)/shard_map/cond/branch_2_fun/ppermute | solution.py:345
  90.9 111.0 %collective-permute-start.8 = (bf16[672,2048]{1,0:T(8,128)(2,1)}, bf16[672,2048]{1,0:T(8,128)(2,1)}, u32[]{:S(2)}, u32[]{:S(2)}) collective-permute-start(bf16[672,2048]{1,0:T(8,128)(2,1)} %slice_bitcast_fusion), channel_id=1, source_target_pairs={{0,32},{8,40},{16,48},{24,56},{32,64},{40,72},{48,80},{56,88},{64,... | collective-permute-start | bytes 8257544 | tf_op jit(solution)/shard_map/cond/branch_2_fun/ppermute | solution.py:345
  121.9 2.7 %copy-start.6 = (bf16[8,768,256]{2,1,0:T(8,128)(2,1)}, bf16[8,768,256]{2,1,0:T(8,128)(2,1)S(1)}, u32[]{:S(2)}) copy-start(bf16[8,768,256]{2,1,0:T(8,128)(2,1)S(1)} %all-to-all-done.11.refs_0_) | copy-start | bytes 9437188 | tf_op jit(solution)/shard_map/cond
  124.6 77.4 %all-to-all-start.10 = ((bf16[8,768,256]{2,1,0:T(8,128)(2,1)}), bf16[8,768,256]{2,1,0:T(8,128)(2,1)}, u32[]{:S(2)}, u32[]{:S(2)}) async-start(bf16[8,768,256]{2,1,0:T(8,128)(2,1)} %broadcast_in_dim.33), calls=%async_computation.10 | async-start | bytes 6291456 | tf_op jit(solution)/shard_map/cond/branch_2_fun/all_to_all | solution.py:332
  132.0 70.0 %collective-permute-start.6 = (bf16[672,768]{1,0:T(8,128)(2,1)S(1)}, bf16[672,768]{1,0:T(8,128)(2,1)S(1)}, u32[]{:S(2)}, u32[]{:S(2)}) collective-permute-start(bf16[672,768]{1,0:T(8,128)(2,1)S(1)} %slice.46), channel_id=1, source_target_pairs={{0,32},{8,40},{16,48},{24,56},{32,64},{40,72},{48,80},{56,88},{64,... | collective-permute-start | bytes 3096584 | tf_op jit(solution)/shard_map/cond/branch_2_fun/ppermute | solution.py:345
  140.4 57.9 %collective-permute-start.9 = (bf16[224,2048]{1,0:T(8,128)(2,1)}, bf16[224,2048]{1,0:T(8,128)(2,1)S(1)}, u32[]{:S(2)}, u32[]{:S(2)}) collective-permute-start(bf16[224,2048]{1,0:T(8,128)(2,1)} %update.16.refs_0_), channel_id=1, source_target_pairs={{0,32},{8,40},{16,48},{24,56},{32,64},{40,72},{48,80},{56,88},{64,... | collective-permute-start | bytes 2752520 | tf_op jit(solution)/shard_map/cond/branch_2_fun/ppermute | solution.py:345
  198.3 0.9 copy-start.18
  202.0 1.0 copy-start.17

commit v2 on v1

--- a/solution.py
+++ b/solution.py
@@ -20,7 +20,7 @@
 PLANS = (
     (0, 0, 224, True, True, False),
     (0, 0, 224, True, True, False),
-    (0, 672, 224, False, False, True),
+    (0, 560, 112, False, False, False),
     (224, 336, 112, False, False, False),
     (0, 384, 128, True, False, False),
 )
@@ -195,13 +195,13 @@
     return jnp.concatenate([one, other], axis=1)
 
 
-def in_pairs(count, body):
-    def both(number, _):
-        body(2 * number)
-        body(2 * number + 1)
+def in_fours(count, body):
+    def four(number, _):
+        for k in range(4):
+            body(4 * number + k)
         return 0
 
-    lax.fori_loop(0, count // 2, both, 0)
+    lax.fori_loop(0, count // 4, four, 0)
 
 
 def update_kernel(rate_ref, hidden_ref, *refs):
@@ -213,7 +213,7 @@
         grad = grad_refs[0][part] if len(grad_refs) == 1 else beside(grad_refs[0][part], grad_refs[1][part])
         updated_ref[:, columns] = updated(rate_ref, hidden_ref, grad, weight_ref[:, columns])
 
-    in_pairs(parts, one_part)
+    in_fours(parts, one_part)
 
 
 def half_update_kernel(half, rate_ref, hidden_ref, grad_ref, weight_ref, updated_ref):
@@ -224,7 +224,7 @@
         weight = beside(*(weight_ref[:, columns_at(4 * pair + 2 * k + half, width)] for k in range(2)))
         updated_ref[:, columns_at(pair, 2 * width)] = updated(rate_ref, hidden_ref, grad, weight)
 
-    in_pairs(parts // 2, one_pair)
+    in_fours(parts // 2, one_pair)
 
 
 def paired_update_kernel(half, rate_ref, hidden_ref, grad_ref, weight_ref, updated_ref):
@@ -234,7 +234,7 @@
         weight = beside(*(weight_ref[:, columns_at(4 * pair + 2 * k + half, width // 2)] for k in range(2)))
         updated_ref[:, columns_at(pair, width)] = updated(rate_ref, hidden_ref, grad_ref[pair], weight)
 
-    in_pairs(pairs, one_pair)
+    in_fours(pairs, one_pair)
 
 
 def update(kernel, rate, hidden_t, grads, weight, first, rows, block, width):
@@ -269,7 +269,7 @@
         peer = updated(rate_ref, hidden_ref, grad_ref[part], weight_ref[:, columns])
         mixed_ref[:, columns] = averaged(own_ref[:, columns], peer)
 
-    in_pairs(parts, one_part)
+    in_fours(parts, one_part)
 
 
 def mix_early(rate, hidden_t, grad, weight, own, first, block, held, rows):
@@ -332,7 +332,10 @@
     return lax.all_to_all(parts, axes, split_axis=0, concat_axis=0, tiled=True)
 
 
-def step(level, gate, up, target, gain, weight, rate):
+SWAP = [(0, 1), (1, 0)]
+
+
+def step(level, prepared, gate, up, target, gain, weight, rate):
     count = lax.axis_size("dp")
     parts = lax.axis_size(TP)
     rows, features = weight.shape
@@ -354,7 +357,7 @@
     if back:
         weight_back = weight[:back]
         peer_weight_back = two_hops(weight_back)
-    hidden_t, coded = forward(gate, up, weight, parts)
+    hidden_t, coded = prepared or forward(gate, up, weight, parts)
     hidden_late = hidden_t
     if early:
         peer_hidden = sent(hidden_t[back:early], by)
@@ -369,15 +372,18 @@
     if early:
         peer_share = sent(grad_share, by)
     pieces = 1 + halves
+    pairs = lax.axis_size("tp_0")
+
+    def with_other(own, other):
+        first = lax.axis_index("tp_1") == 0
+        both = jnp.concatenate([jnp.where(first, own, other), jnp.where(first, other, own)], axis=1)
+        return jnp.broadcast_to(both, (pairs, *both.shape))
+
     if paired:
-        pairs = lax.axis_size("tp_0")
-        other = lax.ppermute(grad_share, "tp_1", [(0, 1), (1, 0)])
-        first = lax.axis_index("tp_1") == 0
+        other = lax.ppermute(grad_share, "tp_1", SWAP)
         piece = width // pieces
         for half in range(pieces):
-            one, two = (x[:, half * piece : (half + 1) * piece] for x in (grad_share, other))
-            both = jnp.concatenate([jnp.where(first, one, two), jnp.where(first, two, one)], axis=1)
-            copies.append(jnp.broadcast_to(both, (pairs, *both.shape)))
+            copies.append(with_other(*(x[:, half * piece : (half + 1) * piece] for x in (grad_share, other))))
     grad = []
     for half in range(pieces):
         grad.append(exchanged(copies[half], "tp_0" if paired else TP))
@@ -419,8 +425,17 @@
     rate = step_rate(round_index).reshape(1)
     levels = lax.axis_size("dp").bit_length() - 1
     level = round_index[0] % levels
-    branches = [functools.partial(step, number) for number in range(levels)]
-    normed, mixed = lax.switch(level, branches, gate_pre, up_pre, target, norm_gain[None], weight[0], rate)
+    operands = (gate_pre, up_pre, target, norm_gain[None], weight[0], rate)
+    last = levels - 1
+
+    def forward_first(*operands):
+        prepared = forward(operands[0], operands[1], operands[4], lax.axis_size(TP))
+        branches = [
+            lambda prepared, operands, number=number: step(number, prepared, *operands) for number in range(last)
+        ]
+        return lax.switch(level, branches, prepared, operands)
+
+    normed, mixed = lax.cond(level == last, functools.partial(step, last, None), forward_first, *operands)
     return normed, mixed[None]
 
 

time: 220 us -> 253 us (1.15)
  waiting for transfers between devices: 77.8 us -> 116 us
  local copies, waits for them, and re-layouts: 11.6 us -> 8.15 us
  loops' own time: 4.05 us -> 0.83 us
    ppermute x4, waiting for transfers between devices: 53.4 us -> 91.6 us  [sent(): lax.ppermute(array, 'dp', [(i, (i + by) % count) for i in range(count)])]
    another operation x1 -> x2, loops' own time: 4.05 us -> 0.83 us  [the longest x1 0.53 us: forward_first(): return lax.switch(level, branches, prepared, operands)]
  transfers between devices with their start and end apart: 6 -> 6, of which waited for: 3 -> 3; matrix products, arithmetic and copies ran while one was open for 4% -> 2% of each run, Pallas kernels for 7% -> 9%
where the time goes in v2:
time: 253 us; the launch traced here: 250 us
  waiting for transfers between devices  116 us (46%)
  blocking collectives  58.1 us (23%)
  Pallas kernels  47.7 us (19%)
  starting transfers between devices  17.6 us (7%)
  local copies, waits for them, and re-layouts  8.15 us (3%)
    ppermute x4, waiting for transfers between devices, sent(): lax.ppermute(array, 'dp', [(i, (i + by) % count) for i in range(count)])  91.6 us
    all_to_all x2, blocking collectives, exchanged(): return lax.all_to_all(parts, axes, split_axis=0, concat_axis=0, tiled=True)  58.1 us
    all_to_all x2, waiting for transfers between devices, exchanged(): return lax.all_to_all(parts, axes, split_axis=0, concat_axis=0, tiled=True)  24.3 us
    pallas_call x2, Pallas kernels, update(): pl.pallas_call(kernel, grid=(rows // block,), in_specs=[pl.BlockSpec(memo...  13.3 us
    all_to_all x2, starting transfers between devices, exchanged(): return lax.all_to_all(parts, axes, split_axis=0, concat_axis=0, tiled=True)  10.7 us
    pallas_call x1, Pallas kernels, forward(): pl.pallas_call(forward_kernel, grid=(tokens // BLOCK,), in_specs=[pl.Bloc...  10.7 us
    pallas_call x1, Pallas kernels, mix_early(): pl.pallas_call(mix_early_kernel, grid=(early // block,), in_specs=[pl.Blo...  8.52 us
    ppermute x4, starting transfers between devices, sent(): lax.ppermute(array, 'dp', [(i, (i + by) % count) for i in range(count)])  6.87 us
  transfers between devices with their start and end apart: 6, of which 3 were waited for; matrix products, arithmetic and copies ran while one was open for 2% of the time, Pallas kernels for 9%

profile of v2, /device:TPU:1, one launch (start us, length us, event | category | flops | bytes accessed | tf_op | source)
XLA Modules:
  0.0 249.8 jit_solution(11948989601476581976)
XLA Ops:
  1.4 248.2 %conditional.2 = ((bf16[768,256]{1,0:T(8,128)(2,1)}, bf16[1,896,2048]{2,1,0:T(8,128)(2,1)})) conditional(s32[]{:T(128)} %convert_element_type.6, (s32[]{:T(128)}, bf16[768,896]{1,0:T(8,128)(2,1)}, bf16[768,896]{1,0:T(8,128)(2,1)}, bf16[896,2048]{1,0:T(8,128)(2,1)}, bf16[768,256]{1,0:T(8,128)(2,1)}, /*index=5*/f32[1,256]{1,0:T(1,128)}, ...), branch_computations={%region_0.5_spmd, %region_5.6_spmd} | conditional | flops 1966085 | bytes 72372992 | solution.py:438
  1.4 0.0 copy-start
  1.4 0.0 copy-start.12
  1.4 10.7 %forward.2 = (bf16[896,768]{1,0:T(8,128)(2,1)S(1)}, s16[8,784,256]{2,1,0:T(8,128)(2,1)}) custom-call(bf16[768,896]{1,0:T(8,128)(2,1)} %get-tuple-element.121.gate_ref, bf16[768,896]{1,0:T(8,128)(2,1)} %get-tuple-element.122.up_ref, bf16[896,2048]{1,0:T(8,128)(2,1)} %get-tuple-element.123.weight_ref), custom_call_target="tpu_custom_call" | custom-call | tf_op jit(solution)/shard_map/cond/branch_0_fun/forward/pallas_call | solution.py:77
  12.1 0.0 copy-done
  12.1 0.0 copy-done.12
  12.1 237.3 %conditional = (bf16[768,256]{1,0:T(8,128)(2,1)}, bf16[1,896,2048]{2,1,0:T(8,128)(2,1)}) conditional(s32[]{:T(128)} %clamp.2, (s16[8,784,256]{2,1,0:T(8,128)(2,1)}, bf16[768,256]{1,0:T(8,128)(2,1)S(1)}, f32[1,256]{1,0:T(1,128)S(1)}, f32[1]{0:T(128)}, bf16[896,768]{1,0:T(8,128)(2,1)S(1)}, ...), branch_computations={%region_1.1_spmd, %region_2.2_spmd, %region_3.3_spmd, %region_4.4_... | conditional | flops 1966084 | bytes 70795760 | solution.py:436
  12.1 46.8 %all_to_all.88.coded_ref.codes_ref = s16[8,784,256]{2,1,0:T(8,128)(2,1)} all-to-all(s16[8,784,256]{2,1,0:T(8,128)(2,1)} %get-tuple-element.98), channel_id=1, replica_groups=mesh['dp'=32,'tp_0'=4,'tp_1'=2] {'tp_0','tp_1'}, dimensions={0} | all-to-all | bytes 6422528 | tf_op jit(solution)/shard_map/cond/branch_0_fun/cond/branch_2_fun/all_to_all | solution.py:332
  58.9 6.0 %share.7 = (f32[768,256]{1,0:T(8,128)}, f32[8,8,768]{2,1,0:T(8,128)}) custom-call(s16[8,784,256]{2,1,0:T(8,128)(2,1)} %all_to_all.88.coded_ref.codes_ref, s16[8,784,256]{2,1,0:T(8,128)(2,1)} %all_to_all.88.coded_ref.codes_ref, bf16[768,256]{1,0:T(8,128)(2,1)S(1)} %get-tuple-element.99.target_ref, f32[1,256]{1,0:T(1,128)S(1)} %get-tuple-element.100.gain_ref), custom_call_target="tpu_custom_call" | custom-call | tf_op jit(solution)/shard_map/cond/branch_0_fun/cond/branch_2_fun/share/pallas_call | solution.py:123
  64.9 11.3 %all_to_all.89.stats_ref = f32[8,8,768]{2,1,0:T(8,128)} all-to-all(f32[8,8,768]{2,1,0:T(8,128)} %get-tuple-element.102), channel_id=1, replica_groups=mesh['dp'=32,'tp_0'=4,'tp_1'=2] {'tp_0','tp_1'}, dimensions={0} | all-to-all | bytes 393216 | tf_op jit(solution)/shard_map/cond/branch_0_fun/cond/branch_2_fun/all_to_all | solution.py:332
  76.3 5.4 %grads.7 = (bf16[768,256]{1,0:T(8,128)(2,1)}, bf16[768,256]{1,0:T(8,128)(2,1)}, bf16[8,768,256]{2,1,0:T(8,128)(2,1)}) custom-call(f32[768,256]{1,0:T(8,128)} %get-tuple-element.101.share_ref, f32[8,8,768]{2,1,0:T(8,128)} %all_to_all.89.stats_ref, bf16[768,256]{1,0:T(8,128)(2,1)S(1)} %get-tuple-element.99.target_ref, f32[1,256]{1,0:T(1,128)S(1)} %get-tuple-element.100.gain_ref), custom_call_target="tpu_custom_call" | custom-call | tf_op jit(solution)/shard_map/cond/branch_0_fun/cond/branch_2_fun/grads/pallas_call | solution.py:170
  81.6 0.0 copy-start.15
  81.6 4.6 %all-to-all-start.2 = ((bf16[8,768,256]{2,1,0:T(8,128)(2,1)}), bf16[8,768,256]{2,1,0:T(8,128)(2,1)}, u32[]{:S(2)}, u32[]{:S(2)}) async-start(bf16[8,768,256]{2,1,0:T(8,128)(2,1)} %get-tuple-element.106), calls=%async_computation.2 | async-start | bytes 6291456 | tf_op jit(solution)/shard_map/cond/branch_0_fun/cond/branch_2_fun/all_to_all | solution.py:332
  86.2 0.0 copy-done.15
  86.2 2.0 collective-permute-start.2
  88.2 10.2 %collective-permute-done.2 = bf16[768,256]{1,0:T(8,128)(2,1)S(1)} collective-permute-done((bf16[768,256]{1,0:T(8,128)(2,1)S(1)}, bf16[768,256]{1,0:T(8,128)(2,1)S(1)}, u32[]{:S(2)}, u32[]{:S(2)}) %collective-permute-start.2) | collective-permute-done | bytes 393248 | tf_op jit(solution)/shard_map/cond/branch_0_fun/cond/branch_2_fun/ppermute | solution.py:348
  98.4 24.3 %all-to-all-done.2.refs_0_ = bf16[8,768,256]{2,1,0:T(8,128)(2,1)} async-done(((bf16[8,768,256]{2,1,0:T(8,128)(2,1)}), bf16[8,768,256]{2,1,0:T(8,128)(2,1)}, u32[]{:S(2)}, u32[]{:S(2)}) %all-to-all-start.2) | async-done | bytes 3145760 | tf_op jit(solution)/shard_map/cond/branch_0_fun/cond/branch_2_fun/all_to_all | solution.py:332
  122.7 1.9 broadcast_in_dim.34
  124.5 6.1 %all-to-all-start.3 = ((bf16[8,768,256]{2,1,0:T(8,128)(2,1)}), bf16[8,768,256]{2,1,0:T(8,128)(2,1)}, u32[]{:S(2)}, u32[]{:S(2)}) async-start(bf16[8,768,256]{2,1,0:T(8,128)(2,1)} %broadcast_in_dim.34), calls=%async_computation.3 | async-start | bytes 6291456 | tf_op jit(solution)/shard_map/cond/branch_0_fun/cond/branch_2_fun/all_to_all | solution.py:332
  130.7 3.3 %slice.48 = bf16[560,2048]{1,0:T(8,128)(2,1)} slice(bf16[896,2048]{1,0:T(8,128)(2,1)} %get-tuple-element.107.refs_1_), slice={[0:560], [0:2048]} | slice | bytes 4587520 | tf_op jit(solution)/shard_map/cond/branch_0_fun/cond/branch_2_fun/slice | solution.py:356
  134.0 1.6 collective-permute-start.3
  135.6 0.9 slice.46.hidden_ref
  136.5 5.8 %update.15.refs_0_ = bf16[336,2048]{1,0:T(8,128)(2,1)} custom-call(f32[1]{0:T(128)S(6)} %mul.14.rate_ref, bf16[448,768]{1,0:T(8,128)(2,1)} %slice.46.hidden_ref, bf16[8,768,256]{2,1,0:T(8,128)(2,1)} %all-to-all-done.2.refs_0_, bf16[896,2048]{1,0:T(8,128)(2,1)} %get-tuple-element.107.refs_1_), custom_call_target="tpu_custom_call" | custom-call | tf_op jit(solution)/shard_map/cond/branch_0_fun/cond/branch_2_fun/update/pallas_call | solution.py:244
  142.3 1.6 collective-permute-start
  143.9 1.0 slice.47
  144.9 1.6 collective-permute-start.1
  146.5 7.6 %update.16.own_ref = bf16[560,2048]{1,0:T(8,128)(2,1)} custom-call(f32[1]{0:T(128)S(6)} %mul.14.rate_ref, bf16[896,768]{1,0:T(8,128)(2,1)S(1)} %get-tuple-element.105.hidden_ref, bf16[8,768,256]{2,1,0:T(8,128)(2,1)} %all-to-all-done.2.refs_0_, bf16[896,2048]{1,0:T(8,128)(2,1)} %get-tuple-element.107.refs_1_), custom_call_target="tpu_custom_call" | custom-call | tf_op jit(solution)/shard_map/cond/branch_0_fun/cond/branch_2_fun/update/pallas_call | solution.py:244
  154.0 81.4 %collective-permute-done.1.hidden_ref = bf16[560,768]{1,0:T(8,128)(2,1)} collective-permute-done((bf16[560,768]{1,0:T(8,128)(2,1)}, bf16[560,768]{1,0:T(8,128)(2,1)}, u32[]{:S(2)}, u32[]{:S(2)}) %collective-permute-start.1) | collective-permute-done | bytes 860192 | tf_op jit(solution)/shard_map/cond/branch_0_fun/cond/branch_2_fun/ppermute | solution.py:348
  235.4 0.0 collective-permute-done.3.weight_ref
  235.4 0.0 all-to-all-done.3.grad_ref
  235.4 8.5 %mix_early.4.refs_2_ = bf16[896,2048]{1,0:T(8,128)(2,1)} custom-call(f32[1]{0:T(128)S(6)} %mul.14.rate_ref, bf16[560,768]{1,0:T(8,128)(2,1)} %collective-permute-done.1.hidden_ref, bf16[8,768,256]{2,1,0:T(8,128)(2,1)} %all-to-all-done.3.grad_ref, bf16[560,2048]{1,0:T(8,128)(2,1)} %collective-permute-done.3.weight_ref, bf16[560,2048]{1,0:T(8,128)(2,1)} %update.16.own_ref), custom_call_target="tpu_custom_call" | custom-call | tf_op jit(solution)/shard_map/cond/branch_0_fun/cond/branch_2_fun/mix_early/pallas_call | solution.py:282
  244.0 0.0 collective-permute-done.refs_1_
  244.0 0.0 copy-start.9
  244.0 1.1 copy-done.9
  245.1 3.8 %mix_late.7 = bf16[896,2048]{1,0:T(8,128)(2,1)} custom-call(bf16[336,2048]{1,0:T(8,128)(2,1)} %update.15.refs_0_, bf16[336,2048]{1,0:T(8,128)(2,1)} %copy-done.9, bf16[896,2048]{1,0:T(8,128)(2,1)} %mix_early.4.refs_2_), custom_call_target="tpu_custom_call", output_to_operand_aliasing={{}: (2, {})} | custom-call | tf_op jit(solution)/shard_map/cond/branch_0_fun/cond/branch_2_fun/mix_late/pallas_call | solution.py:320
Async XLA Ops:
  1.4 10.7 %copy-start = (bf16[768,256]{1,0:T(8,128)(2,1)S(1)}, bf16[768,256]{1,0:T(8,128)(2,1)}, u32[]{:S(2)}) copy-start(bf16[768,256]{1,0:T(8,128)(2,1)} %get-tuple-element.125) | copy-start | bytes 1179652 | tf_op jit(solution)/shard_map/cond
  1.4 10.7 %copy-start.12 = (f32[1,256]{1,0:T(1,128)S(1)}, f32[1,256]{1,0:T(1,128)}, u32[]{:S(2)}) copy-start(f32[1,256]{1,0:T(1,128)} %get-tuple-element.126) | copy-start | bytes 3076 | tf_op jit(solution)/shard_map/cond
  81.6 4.6 %copy-start.15 = (bf16[768,256]{1,0:T(8,128)(2,1)S(1)}, bf16[768,256]{1,0:T(8,128)(2,1)}, u32[]{:S(2)}) copy-start(bf16[768,256]{1,0:T(8,128)(2,1)} %get-tuple-element.108) | copy-start | bytes 1179652 | tf_op jit(solution)/shard_map/cond/branch_0_fun/cond
  81.6 41.0 %all-to-all-start.2 = ((bf16[8,768,256]{2,1,0:T(8,128)(2,1)}), bf16[8,768,256]{2,1,0:T(8,128)(2,1)}, u32[]{:S(2)}, u32[]{:S(2)}) async-start(bf16[8,768,256]{2,1,0:T(8,128)(2,1)} %get-tuple-element.106), calls=%async_computation.2 | async-start | bytes 6291456 | tf_op jit(solution)/shard_map/cond/branch_0_fun/cond/branch_2_fun/all_to_all | solution.py:332
  86.2 12.2 %collective-permute-start.2 = (bf16[768,256]{1,0:T(8,128)(2,1)S(1)}, bf16[768,256]{1,0:T(8,128)(2,1)S(1)}, u32[]{:S(2)}, u32[]{:S(2)}) collective-permute-start(bf16[768,256]{1,0:T(8,128)(2,1)S(1)} %copy-done.15), channel_id=1, source_target_pairs={{0,32},{8,40},{16,48},{24,56},{32,64},{40,72},{48,80},{56,88},{64,... | collective-permute-start | bytes 1179656 | tf_op jit(solution)/shard_map/cond/branch_0_fun/cond/branch_2_fun/ppermute | solution.py:348
  124.5 110.9 %all-to-all-start.3 = ((bf16[8,768,256]{2,1,0:T(8,128)(2,1)}), bf16[8,768,256]{2,1,0:T(8,128)(2,1)}, u32[]{:S(2)}, u32[]{:S(2)}) async-start(bf16[8,768,256]{2,1,0:T(8,128)(2,1)} %broadcast_in_dim.34), calls=%async_computation.3 | async-start | bytes 6291456 | tf_op jit(solution)/shard_map/cond/branch_0_fun/cond/branch_2_fun/all_to_all | solution.py:332
  134.0 101.5 %collective-permute-start.3 = (bf16[560,2048]{1,0:T(8,128)(2,1)}, bf16[560,2048]{1,0:T(8,128)(2,1)}, u32[]{:S(2)}, u32[]{:S(2)}) collective-permute-start(bf16[560,2048]{1,0:T(8,128)(2,1)} %slice.48), channel_id=1, source_target_pairs={{0,32},{8,40},{16,48},{24,56},{32,64},{40,72},{48,80},{56,88},{64,... | collective-permute-start | bytes 6881288 | tf_op jit(solution)/shard_map/cond/branch_0_fun/cond/branch_2_fun/ppermute | solution.py:348
  142.3 101.7 %collective-permute-start = (bf16[336,2048]{1,0:T(8,128)(2,1)}, bf16[336,2048]{1,0:T(8,128)(2,1)S(1)}, u32[]{:S(2)}, u32[]{:S(2)}) collective-permute-start(bf16[336,2048]{1,0:T(8,128)(2,1)} %update.15.refs_0_), channel_id=1, source_target_pairs={{0,32},{8,40},{16,48},{24,56},{32,64},{40,72},{48,80},{56,88},{64,... | collective-permute-start | bytes 4128776 | tf_op jit(solution)/shard_map/cond/branch_0_fun/cond/branch_2_fun/ppermute | solution.py:348
  144.9 90.6 %collective-permute-start.1 = (bf16[560,768]{1,0:T(8,128)(2,1)}, bf16[560,768]{1,0:T(8,128)(2,1)}, u32[]{:S(2)}, u32[]{:S(2)}) collective-permute-start(bf16[560,768]{1,0:T(8,128)(2,1)} %slice.47), channel_id=1, source_target_pairs={{0,32},{8,40},{16,48},{24,56},{32,64},{40,72},{48,80},{56,88},{64,... | collective-permute-start | bytes 2580488 | tf_op jit(solution)/shard_map/cond/branch_0_fun/cond/branch_2_fun/ppermute | solution.py:348
  244.0 1.1 copy-start.9
